TPU v7x, 256 devices: a whole 4x4x8 slice. The times are simulated.
256 devices in a mesh: expert: 64 (over z, y, core), dp: 4 (over x).
Axes of the slice: x: 4, y: 4, z: 8, core: 2. Of those that a mesh axis runs over, the one named last changes fastest.
Arguments:
- tokens: bfloat16 [16384, 2880], P(('expert', 'dp')), may hold values from -6 to 6
- expert_ids: int32 [16384, 4], P(('expert', 'dp')), may hold values from 0 to 63, all different within a row; in each aligned block of 64 rows (0 to 63, 64 to 127, ...) at most 6 rows name the same one
- gate_logits: float32 [16384, 4], P(('expert', 'dp')), may hold values from -3 to 3
- w_gate: bfloat16 [64, 2880, 1536], P('expert', None, 'dp'), may hold values from -0.109375 to 0.109375
- w_up: bfloat16 [64, 2880, 1536], P('expert', None, 'dp'), may hold values from -0.109375 to 0.109375
- w_down: bfloat16 [64, 1536, 2880], P('expert', 'dp'), may hold values from -0.15625 to 0.15625
Outputs:
- mixed: bfloat16 [16384, 2880], P(('expert', 'dp'))
Inputs may be any that keep to these rules, and one draw needn't show every extreme that they name: `expert_ids`: each row names 4 different experts. Among the 64 rows of one device no expert is named more than 6 times, and every expert is named somewhere.
All inputs are finite; a program needn't handle non-finite values.
Results may differ from a plain program's by a relative error of at most 0.012.
Values may be sent and summed in bfloat16 or wider, within the bound.
No kernel may reach another device: no remote copies, remote signals or barrier semaphores. Data moves between devices by JAX's collectives and lax.ppermute only.
A program may use at most 128 MiB of HBM per device.

v0:
```python
import jax
import jax.numpy as jnp
from jax import lax
from jax.sharding import PartitionSpec as P


def expert_rows(tile_in, gate_w, up_w, down_w):
    gate_val = jnp.dot(tile_in, gate_w, preferred_element_type=jnp.float32)
    up_val = jnp.dot(tile_in, up_w, preferred_element_type=jnp.float32)
    hidden = ((up_val + 1.0) * gate_val * jax.nn.sigmoid(1.702 * gate_val)).astype(jnp.bfloat16)
    return jnp.dot(hidden, down_w, preferred_element_type=jnp.float32).astype(jnp.bfloat16)


def run_tiles(packed, first_row, last_row, gate_w, up_w, down_w):
    tile_rows = 128
    n_tiles = jnp.maximum(last_row - first_row + tile_rows - 1, 0) // tile_rows
    result_buf = jnp.zeros((packed.shape[0], down_w.shape[1]), jnp.bfloat16)

    def advance(index_t, buffer):
        at_row = first_row + index_t * tile_rows
        tile_in = lax.dynamic_slice_in_dim(packed, at_row, tile_rows, 0)
        return lax.dynamic_update_slice_in_dim(
            buffer, expert_rows(tile_in, gate_w, up_w, down_w), at_row, 0
        )

    return lax.fori_loop(0, n_tiles, advance, result_buf)


def per_device(tokens, expert_ids, gate_logits, w_gate, w_up, w_down):
    n_rows, width = tokens.shape
    n_tops = expert_ids.shape[1]
    n_exp = lax.axis_size("expert")
    n_dp = lax.axis_size("dp")
    slot_cap = max(2, 3 * n_rows * n_tops // (2 * n_exp))
    tile_rows = 128
    flat_ids = expert_ids.reshape(-1)
    onehot = (flat_ids[:, None] == jnp.arange(n_exp, dtype=jnp.int32)[None, :]).astype(jnp.int32)
    rank_in = jnp.sum((jnp.cumsum(onehot, axis=0) - onehot) * onehot, axis=1)
    counts = jnp.sum(onehot, axis=0)
    slot_idx = flat_ids * slot_cap + rank_in
    source = (
        jnp.zeros((n_exp * slot_cap,), jnp.int32)
        .at[slot_idx]
        .set(jnp.arange(n_rows * n_tops, dtype=jnp.int32) // n_tops)
    )
    filled = (jnp.arange(slot_cap)[None, :] < counts[:, None]).reshape(-1)
    outgoing = jnp.where(filled[:, None], tokens[source], jnp.zeros_like(tokens[source])).reshape(
        n_exp, slot_cap, width
    )
    rows_mid, counts_mid = (
        lax.all_to_all(outgoing, "expert", split_axis=0, concat_axis=0, tiled=True),
        lax.all_to_all(counts[:, None], "expert", split_axis=0, concat_axis=0, tiled=True),
    )
    rows_in, counts_in = (
        lax.all_gather(rows_mid, "dp", axis=0, tiled=True),
        lax.all_gather(counts_mid, "dp", axis=0, tiled=True),
    )
    rows_flat = rows_in.reshape(-1, width)
    total_rows = rows_flat.shape[0]
    live_row = (jnp.arange(slot_cap)[None, :] < counts_in.reshape(-1)[:, None]).reshape(-1)
    position = jnp.cumsum(live_row.astype(jnp.int32)) - 1
    live_total = jnp.sum(live_row.astype(jnp.int32))
    padded = (total_rows + tile_rows - 1) // tile_rows * tile_rows + tile_rows
    gather_idx = (
        jnp.zeros((padded,), jnp.int32)
        .at[jnp.where(live_row, position, padded)]
        .set(jnp.arange(total_rows, dtype=jnp.int32), mode="drop")
    )
    packed = rows_flat[gather_idx]
    gate_w = w_gate[0]
    up_w = w_up[0]
    down_w = w_down[0]
    merged = run_tiles(packed, 0, live_total, gate_w, up_w, down_w)
    slot_out = jnp.where(
        live_row[:, None],
        merged[jnp.where(live_row, position, 0)],
        jnp.zeros((total_rows, width), jnp.bfloat16),
    )
    summed = lax.psum_scatter(
        slot_out.reshape(n_dp * n_exp, slot_cap, width), "dp", scatter_dimension=0, tiled=True
    ).astype(jnp.float32)
    expert_out = lax.all_to_all(
        summed.astype(jnp.bfloat16), "expert", split_axis=0, concat_axis=0, tiled=True
    )
    picked = expert_out.reshape(n_exp * slot_cap, width)[slot_idx]
    gate_wts = jnp.exp(gate_logits)
    gate_wts = gate_wts / jnp.sum(gate_wts, axis=1, keepdims=True)
    mixed = jnp.sum(
        picked.reshape(n_rows, n_tops, width).astype(jnp.float32) * gate_wts[:, :, None], axis=1
    )
    return mixed.astype(jnp.bfloat16)


def solution(mesh):
    return jax.shard_map(
        per_device,
        mesh=mesh,
        in_specs=(
            P(("expert", "dp"), None),
            P(("expert", "dp"), None),
            P(("expert", "dp"), None),
            P("expert", None, "dp"),
            P("expert", None, "dp"),
            P("expert", "dp", None),
        ),
        out_specs=P(("expert", "dp"), None),
        check_vma=False,
    )
```

profile of v0, /device:TPU:8, one launch (start us, length us, event | category | flops | bytes accessed | tf_op | source)
XLA Modules:
  0.0 599.4 jit_solution(584529033476823874)
XLA Ops:
  6.5 0.8 copy.27
  7.6 0.7 broadcast_multiply_fusion
  8.3 0.6 reduce-window.15
  9.5 1.4 scatter_custom_fusion
  10.9 3.5 gather_fusion
  14.4 2.8 gather.17
  17.6 82.8 %all_to_all.22 = bf16[64,6,2880]{2,1,0:T(8,128)(2,1)S(1)} all-to-all(bf16[64,6,2880]{2,1,0:T(8,128)(2,1)S(1)} %broadcast_select_fusion.1), channel_id=1, replica_groups=mesh['expert'=64,'dp'=4] {'expert'}, dimensions={0} | all-to-all | bytes 4423680 | tf_op jit(solution)/shard_map/all_to_all | solution.py:51
  100.4 1.7 copy.32
  102.1 0.7 copy.28
  102.8 5.7 all-to-all-start
  108.6 3.0 copy.34
  111.7 0.6 dynamic-slice
  112.9 4.2 all-to-all-done
  117.1 1.2 reduce.1
  118.6 9.3 %all-reduce = s32[256]{0:T(256)S(1)} all-reduce(s32[256]{0:T(256)S(1)} %dynamic-update-slice), channel_id=2, replica_groups=mesh['expert'=64,'dp'=4] {'dp'}, use_global_device_ids=true, to_apply=%add | all-reduce | flops 256 | bytes 2048
  127.9 0.7 convert_reduce_fusion.1
  130.3 6.4 %scatter_custom_fusion.1 = s32[1664]{0:T(1024)S(1)} fusion(s32[1536]{0:T(1024)S(1)} %get-tuple-element.45, s32[1536]{0:T(1024)S(1)} %iota.22, s32[]{:T(128)} %constant.65.clone.1), kind=kCustom, calls=%fused_computation.57 | custom fusion | bytes 6660 | tf_op jit(solution)/shard_map/scatter | solution.py:67
  136.8 53.3 %all-gather.3.cloned.1.call-done = bf16[256,6,2880]{2,0,1:T(8,128)(2,1)} async-done(((bf16[64,6,2880]{2,0,1:T(8,128)(2,1)}), bf16[256,6,2880]{2,0,1:T(8,128)(2,1)}) %all-gather.3.cloned.1.call-update) | async-done | bytes 8847376 | tf_op jit(solution)/shard_map/all_gather | solution.py:55
  190.1 12.9 %copy.33 = bf16[256,6,2880]{2,1,0:T(8,128)(2,1)} copy(bf16[256,6,2880]{2,0,1:T(8,128)(2,1)} %all-gather.3.cloned.1.call-done) | data formatting | bytes 17694720 | tf_op jit(solution)/shard_map/all_gather | solution.py:55
  203.0 15.1 %reshape.195 = bf16[1536,2880]{1,0:T(8,128)(2,1)} reshape(bf16[256,6,2880]{2,1,0:T(8,128)(2,1)} %copy.33) | data formatting | bytes 17694720 | tf_op jit(solution)/shard_map/reshape | solution.py:58
  218.1 24.0 %gather_fusion.1 = bf16[1664,2880]{1,0:T(8,128)(2,1)} fusion(bf16[1536,2880]{1,0:T(8,128)(2,1)} %reshape.195, s32[2048]{0:T(1024)S(1)} %pad_clamp_fusion.1), kind=kCustom, calls=%fused_computation.1 | custom fusion | bytes 19175936 | tf_op jit(solution)/shard_map/gather | solution.py:69
  242.1 4.3 broadcast_in_dim.48
  246.4 45.9 %while.10 = (s32[]{:T(128)}, bf16[1664,2880]{0,1:T(8,128)(2,1)}, s32[]{:T(128)}, bf16[1664,2880]{1,0:T(8,128)(2,1)}, bf16[2880,384]{1,0:T(8,128)(2,1)}, /*index=...) while((s32[]{:T(128)}, bf16[1664,2880]{0,1:T(8,128)(2,1)}, ...), condition=%wide.region_10.11_spmd, body=%wide.region_9.10_spmd.sunk | while | flops 850108416 | bytes 9274527 | solution.py:26
  246.4 2.4 fusion.45
  248.8 4.1 fusion.46
  253.0 2.4 fusion.45
  255.4 4.2 fusion.46
  259.5 2.4 fusion.45
  261.9 4.1 fusion.46
  266.1 2.4 fusion.45
  268.5 4.2 fusion.46
  272.7 2.4 fusion.45
  275.1 4.1 fusion.46
  279.2 2.4 fusion.45
  281.6 4.1 fusion.46
  285.8 2.4 fusion.45
  288.2 4.1 fusion.46
  292.3 14.0 %copy.35 = bf16[1664,2880]{1,0:T(8,128)(2,1)} copy(bf16[1664,2880]{0,1:T(8,128)(2,1)} %get-tuple-element.43) | data formatting | bytes 19169280 | tf_op jit(solution)/shard_map/while | solution.py:26
  306.3 21.9 %gather_fusion.2 = bf16[1536,2880]{1,0:T(8,128)(2,1)} fusion(bf16[1664,2880]{1,0:T(8,128)(2,1)} %copy.35, s32[2048]{0:T(1024)S(1)} %pad_clamp_fusion), kind=kCustom, calls=%fused_computation.2 | custom fusion | bytes 17700864 | tf_op jit(solution)/shard_map/gather | solution.py:76
  328.3 13.9 %gather.20 = bf16[256,6,2880]{2,1,0:T(8,128)(2,1)} reshape(bf16[1536,2880]{1,0:T(8,128)(2,1)} %gather_fusion.2) | data formatting | bytes 17694720 | tf_op jit(solution)/shard_map/gather | solution.py:76
  342.2 10.6 %broadcast_select_fusion = bf16[256,6,2880]{2,1,0:T(8,128)(2,1)} fusion(bf16[256,6,2880]{2,1,0:T(8,128)(2,1)} %gather.20, pred[256,6]{1,0:T(8,128)(4,1)S(1)} %get-tuple-element.63), kind=kLoop, calls=%fused_computation.26 | loop fusion | flops 4423680 | bytes 17696256 | tf_op jit(solution)/shard_map/jit(_where)/select_n | solution.py:74
  352.9 146.5 %reduce-scatter.2.cloned.1.call-done = bf16[64,6,2880]{2,1,0:T(8,128)(2,1)} async-done(((bf16[256,6,2880]{2,1,0:T(8,128)(2,1)}), bf16[64,6,2880]{2,1,0:T(8,128)(2,1)}) %reduce-scatter.2.cloned.1.call-update) | async-done | bytes 2211856 | tf_op jit(solution)/shard_map/reduce_scatter | solution.py:79
  499.4 10.7 %all-to-all-start.2 = ((bf16[64,6,2880]{2,1,0:T(8,128)(2,1)}), bf16[64,6,2880]{2,1,0:T(8,128)(2,1)}, u32[]{:S(2)}, u32[]{:S(2)}) async-start(bf16[64,6,2880]{2,1,0:T(8,128)(2,1)} %reduce-scatter.2.cloned.1.call-done), calls=%async_computation.3 | async-start | bytes 6029312 | tf_op jit(solution)/shard_map/all_to_all | solution.py:82
  510.3 70.7 %all-to-all-done.2 = bf16[64,6,2880]{2,1,0:T(8,128)(2,1)} async-done(((bf16[64,6,2880]{2,1,0:T(8,128)(2,1)}), bf16[64,6,2880]{2,1,0:T(8,128)(2,1)}, u32[]{:S(2)}, u32[]{:S(2)}) %all-to-all-start.2) | async-done | bytes 2211872 | tf_op jit(solution)/shard_map/all_to_all | solution.py:82
  580.9 3.3 reshape.197
  584.3 2.7 gather_fusion.3
  587.0 2.8 reshape.199
  589.8 2.8 multiply_reduce_fusion
  (46 shorter events, 2.8 us)
Async XLA Ops:
  6.5 4.4 copy-start
  6.5 183.6 %all-gather.3.cloned.1.call-start = ((), (), s32[]{:S(2)}) async-start(), calls=%async_computation.4 | async-start | bytes 11304960 | tf_op jit(solution)/shard_map/all_gather | solution.py:55
  102.1 9.6 %copy-start.3 = (u32[256]{0:T(256)S(1)}, u32[256]{0:T(256)}, u32[]{:S(2)}) copy-start(u32[256]{0:T(256)} %constant.87) | copy-start | bytes 3076
  102.8 14.3 %all-to-all-start = ((s32[64,1,1]{2,1,0:T(1,128)}), s32[64,1,1]{2,1,0:T(1,128)S(1)}, u32[]{:S(2)}, u32[]{:S(2)}) async-start(s32[64,1,1]{2,1,0:T(1,128)} %copy.28), calls=%async_computation | async-start | bytes 65536 | tf_op jit(solution)/shard_map/all_to_all | solution.py:52
  108.6 390.8 %reduce-scatter.2.cloned.1.call-start = ((), (), s32[]{:S(2)}) async-start(), calls=%async_computation.5 | async-start | bytes 15073280 | tf_op jit(solution)/shard_map/reduce_scatter | solution.py:79
  352.8 157.3 %copy-start.2 = (f32[64,4]{0,1:T(4,128)S(1)}, f32[64,4]{0,1:T(4,128)}, u32[]{:S(2)}) copy-start(f32[64,4]{0,1:T(4,128)} %param.10) | copy-start | bytes 3076
  499.4 81.6 %all-to-all-start.2 = ((bf16[64,6,2880]{2,1,0:T(8,128)(2,1)}), bf16[64,6,2880]{2,1,0:T(8,128)(2,1)}, u32[]{:S(2)}, u32[]{:S(2)}) async-start(bf16[64,6,2880]{2,1,0:T(8,128)(2,1)} %reduce-scatter.2.cloned.1.call-done), calls=%async_computation.3 | async-start | bytes 6029312 | tf_op jit(solution)/shard_map/all_to_all | solution.py:82
  584.3 8.3 %copy-start.1 = (bf16[64,2880]{1,0:T(8,128)(2,1)S(1)}, bf16[64,2880]{1,0:T(8,128)(2,1)}, u32[]{:S(2)}) copy-start(bf16[64,2880]{1,0:T(8,128)(2,1)} %param.8) | copy-start | bytes 1105924
Sparse Core Ops, SparseCore 0:
  102.3 87.7 all-gather.2
  353.0 146.3 reduce-scatter.1
where the time goes:
time: 602 us; the launch traced here: 599 us
  waiting for transfers between devices  275 us (46%)
  local copies, waits for them, and re-layouts  137 us (23%)
  blocking collectives  92.1 us (15%)
  matrix products  45.8 us (8%)
  other arithmetic  17.9 us (3%)
  starting transfers between devices  16.5 us (3%)
  between operations  15 us (2%)
    reduce_scatter x1, waiting for transfers between devices, per_device(): lax.psum_scatter(slot_out.reshape(n_dp * n_exp, slot_cap, width), 'dp', s...  147 us
    all_to_all x1, blocking collectives, per_device(): lax.all_to_all(outgoing, 'expert', split_axis=0, concat_axis=0, tiled=True)  82.8 us
    all_to_all x1, waiting for transfers between devices, per_device(): lax.all_to_all(summed.astype(jnp.bfloat16), 'expert', split_axis=0, conca...  70.7 us
    all_gather x1, waiting for transfers between devices, per_device(): lax.all_gather(rows_mid, 'dp', axis=0, tiled=True)  53.3 us
    gather x2, local copies, waits for them, and re-layouts, per_device(): merged[jnp.where(live_row, position, 0)]  35.8 us
    dot_general x7, matrix products, expert_rows(): jnp.dot(hidden, down_w, preferred_element_type=jnp.float32)  29 us
    gather x1, local copies, waits for them, and re-layouts, per_device(): packed = rows_flat[gather_idx]  24 us
    dot_general x7, matrix products, expert_rows(): gate_val = jnp.dot(tile_in, gate_w, preferred_element_type=jnp.float32)  16.9 us
  transfers between devices with their start and end apart: 4, of which 4 were waited for; matrix products, arithmetic and copies ran while one was open for 2% of the time, Pallas kernels for 0%

commit v1 on v0

--- a/solution.py
+++ b/solution.py
@@ -2,6 +2,12 @@
 import jax.numpy as jnp
 from jax import lax
 from jax.sharding import PartitionSpec as P
+
+
+def gather_from_all(x, axis, dim):
+    peers = lax.axis_size(axis)
+    repeats = [peers if d == dim else 1 for d in range(x.ndim)]
+    return lax.all_to_all(jnp.tile(x, repeats), axis, split_axis=dim, concat_axis=dim, tiled=True)
 
 
 def expert_rows(tile_in, gate_w, up_w, down_w):
@@ -52,7 +58,7 @@
         lax.all_to_all(counts[:, None], "expert", split_axis=0, concat_axis=0, tiled=True),
     )
     rows_in, counts_in = (
-        lax.all_gather(rows_mid, "dp", axis=0, tiled=True),
+        gather_from_all(rows_mid, "dp", 0),
         lax.all_gather(counts_mid, "dp", axis=0, tiled=True),
     )
     rows_flat = rows_in.reshape(-1, width)

time: 602 us -> 662 us (1.100)
  blocking collectives: 92.1 us -> 211 us
  waiting for transfers between devices: 275 us -> 211 us
  starting transfers between devices: 16.5 us -> 29.3 us
  local copies, waits for them, and re-layouts: 137 us -> 128 us
    unnamed x1, blocking collectives: 9.3 us -> 130 us
    all_gather x1 -> x0, waiting for transfers between devices: 53.3 us -> none  [per_device(): lax.all_gather(rows_mid, 'dp', axis=0, tiled=True)]
    all_gather x1 -> x0, local copies, waits for them, and re-layouts: 12.9 us -> none  [per_device(): lax.all_gather(rows_mid, 'dp', axis=0, tiled=True)]
  transfers between devices with their start and end apart: 4 -> 4, of which waited for: 4 -> 2; matrix products, arithmetic and copies ran while one was open for 2% -> 4% of each run, Pallas kernels for 0% -> 0%
where the time goes in v1:
time: 662 us; the launch traced here: 660 us
  waiting for transfers between devices  211 us (32%)
  blocking collectives  211 us (32%)
  local copies, waits for them, and re-layouts  128 us (19%)
  matrix products  45.8 us (7%)
  starting transfers between devices  29.3 us (4%)
  other arithmetic  19.5 us (3%)
  between operations  14.9 us (2%)
    reduce_scatter x1, waiting for transfers between devices, per_device(): lax.psum_scatter(slot_out.reshape(n_dp * n_exp, slot_cap, width), 'dp', s...  140 us
    unnamed x1, blocking collectives  130 us
    all_to_all x1, blocking collectives, per_device(): lax.all_to_all(outgoing, 'expert', split_axis=0, concat_axis=0, tiled=True)  81.2 us
    all_to_all x1, waiting for transfers between devices, per_device(): lax.all_to_all(summed.astype(jnp.bfloat16), 'expert', split_axis=0, conca...  70.7 us
    gather x2, local copies, waits for them, and re-layouts, per_device(): merged[jnp.where(live_row, position, 0)]  35.8 us
    dot_general x7, matrix products, expert_rows(): jnp.dot(hidden, down_w, preferred_element_type=jnp.float32)  29 us
    gather x1, local copies, waits for them, and re-layouts, per_device(): packed = rows_flat[gather_idx]  24 us
    dot_general x7, matrix products, expert_rows(): gate_val = jnp.dot(tile_in, gate_w, preferred_element_type=jnp.float32)  16.9 us
  transfers between devices with their start and end apart: 4, of which 2 were waited for; matrix products, arithmetic and copies ran while one was open for 4% of the time, Pallas kernels for 0%

profile of v1, /device:TPU:8, one launch (start us, length us, event | category | flops | bytes accessed | tf_op | source)
XLA Modules:
  0.0 659.6 jit_solution(6524451152656927642)
XLA Ops:
  6.5 0.8 copy.25
  7.6 0.6 reduce-window.15
  8.6 0.7 copy.26
  9.3 12.1 %all-to-all-start = ((s32[64,1,1]{2,1,0:T(1,128)}), s32[64,1,1]{2,1,0:T(1,128)S(1)}, u32[]{:S(2)}, u32[]{:S(2)}) async-start(s32[64,1,1]{2,1,0:T(1,128)} %copy.26), calls=%async_computation | async-start | bytes 65536 | tf_op jit(solution)/shard_map/all_to_all | solution.py:58
  21.4 0.7 broadcast_multiply_fusion
  22.4 1.4 scatter_custom_fusion
  23.8 3.5 gather_fusion
  27.3 2.8 gather.17
  30.1 2.0 broadcast_select_fusion.1
  32.1 81.2 %all_to_all.27 = bf16[64,6,2880]{2,1,0:T(8,128)(2,1)S(1)} all-to-all(bf16[64,6,2880]{2,1,0:T(8,128)(2,1)} %broadcast_select_fusion.1), channel_id=1, replica_groups=mesh['expert'=64,'dp'=4] {'expert'}, dimensions={0} | all-to-all | bytes 4423680 | tf_op jit(solution)/shard_map/all_to_all | solution.py:57
  113.3 5.2 tile.4
  118.5 6.2 all-to-all-start.2
  124.8 2.9 copy.30
  127.7 0.6 dynamic-slice
  128.9 1.2 reduce.1
  130.4 129.9 %all-reduce = s32[256]{0:T(256)S(1)} all-reduce(s32[256]{0:T(256)S(1)} %dynamic-update-slice), channel_id=2, replica_groups=mesh['expert'=64,'dp'=4] {'dp'}, use_global_device_ids=true, to_apply=%add | all-reduce | flops 256 | bytes 2048
  260.3 0.7 convert_reduce_fusion.1
  261.8 0.3 reduce-window.19
  262.7 6.4 scatter_custom_fusion.1
  269.1 15.1 %reshape.199 = bf16[1536,2880]{1,0:T(8,128)(2,1)} reshape(bf16[256,6,2880]{2,1,0:T(8,128)(2,1)} %all-to-all-done.2) | data formatting | bytes 17694720 | tf_op jit(solution)/shard_map/reshape | solution.py:64
  284.2 24.0 %gather_fusion.1 = bf16[1664,2880]{1,0:T(8,128)(2,1)} fusion(bf16[1536,2880]{1,0:T(8,128)(2,1)} %reshape.199, s32[2048]{0:T(1024)S(1)} %pad_clamp_fusion.1), kind=kCustom, calls=%fused_computation.1 | custom fusion | bytes 19175936 | tf_op jit(solution)/shard_map/gather | solution.py:75
  308.2 4.3 broadcast_in_dim.48
  312.5 45.9 %while.10 = (s32[]{:T(128)}, bf16[1664,2880]{0,1:T(8,128)(2,1)}, s32[]{:T(128)}, bf16[1664,2880]{1,0:T(8,128)(2,1)}, bf16[2880,384]{1,0:T(8,128)(2,1)}, /*index=...) while((s32[]{:T(128)}, bf16[1664,2880]{0,1:T(8,128)(2,1)}, ...), condition=%wide.region_10.11_spmd, body=%wide.region_9.10_spmd.sunk | while | flops 850108416 | bytes 9274527 | solution.py:32
  312.5 2.4 fusion.45
  314.9 4.1 fusion.46
  319.1 2.4 fusion.45
  321.5 4.2 fusion.46
  325.6 2.4 fusion.45
  328.1 4.1 fusion.46
  332.2 2.4 fusion.45
  334.6 4.2 fusion.46
  338.8 2.4 fusion.45
  341.2 4.1 fusion.46
  345.3 2.4 fusion.45
  347.7 4.1 fusion.46
  351.9 2.4 fusion.45
  354.3 4.1 fusion.46
  358.4 14.0 %copy.31 = bf16[1664,2880]{1,0:T(8,128)(2,1)} copy(bf16[1664,2880]{0,1:T(8,128)(2,1)} %get-tuple-element.43) | data formatting | bytes 19169280 | tf_op jit(solution)/shard_map/while | solution.py:32
  372.5 21.9 %gather_fusion.2 = bf16[1536,2880]{1,0:T(8,128)(2,1)} fusion(bf16[1664,2880]{1,0:T(8,128)(2,1)} %copy.31, s32[2048]{0:T(1024)S(1)} %pad_clamp_fusion), kind=kCustom, calls=%fused_computation.2 | custom fusion | bytes 17700864 | tf_op jit(solution)/shard_map/gather | solution.py:82
  394.4 13.9 %gather.20 = bf16[256,6,2880]{2,1,0:T(8,128)(2,1)} reshape(bf16[1536,2880]{1,0:T(8,128)(2,1)} %gather_fusion.2) | data formatting | bytes 17694720 | tf_op jit(solution)/shard_map/gather | solution.py:82
  408.3 10.6 %broadcast_select_fusion = bf16[256,6,2880]{2,1,0:T(8,128)(2,1)} fusion(bf16[256,6,2880]{2,1,0:T(8,128)(2,1)} %gather.20, pred[256,6]{1,0:T(8,128)(4,1)S(1)} %get-tuple-element.63), kind=kLoop, calls=%fused_computation.26 | loop fusion | flops 4423680 | bytes 17696256 | tf_op jit(solution)/shard_map/jit(_where)/select_n | solution.py:80
  419.0 140.4 %reduce-scatter.2.cloned.1.call-done = bf16[64,6,2880]{2,1,0:T(8,128)(2,1)} async-done(((bf16[256,6,2880]{2,1,0:T(8,128)(2,1)}), bf16[64,6,2880]{2,1,0:T(8,128)(2,1)}) %reduce-scatter.2.cloned.1.call-update) | async-done | bytes 2211856 | tf_op jit(solution)/shard_map/reduce_scatter | solution.py:85
  559.3 11.0 %all-to-all-start.3 = ((bf16[64,6,2880]{2,1,0:T(8,128)(2,1)}), bf16[64,6,2880]{2,1,0:T(8,128)(2,1)}, u32[]{:S(2)}, u32[]{:S(2)}) async-start(bf16[64,6,2880]{2,1,0:T(8,128)(2,1)} %reduce-scatter.2.cloned.1.call-done), calls=%async_computation.4 | async-start | bytes 6029312 | tf_op jit(solution)/shard_map/all_to_all | solution.py:88
  570.4 70.7 %all-to-all-done.3 = bf16[64,6,2880]{2,1,0:T(8,128)(2,1)} async-done(((bf16[64,6,2880]{2,1,0:T(8,128)(2,1)}), bf16[64,6,2880]{2,1,0:T(8,128)(2,1)}, u32[]{:S(2)}, u32[]{:S(2)}) %all-to-all-start.3) | async-done | bytes 2211872 | tf_op jit(solution)/shard_map/all_to_all | solution.py:88
  641.1 3.3 reshape.201
  644.5 2.7 gather_fusion.3
  647.2 2.8 reshape.203
  650.0 2.8 multiply_reduce_fusion
  (44 shorter events, 2.1 us)
Async XLA Ops:
  6.5 17.3 %copy-start = (bf16[64,2880]{1,0:T(8,128)(2,1)S(1)}, bf16[64,2880]{1,0:T(8,128)(2,1)}, u32[]{:S(2)}) copy-start(bf16[64,2880]{1,0:T(8,128)(2,1)} %param.8) | copy-start | bytes 1105924
  9.3 22.8 %all-to-all-start = ((s32[64,1,1]{2,1,0:T(1,128)}), s32[64,1,1]{2,1,0:T(1,128)S(1)}, u32[]{:S(2)}, u32[]{:S(2)}) async-start(s32[64,1,1]{2,1,0:T(1,128)} %copy.26), calls=%async_computation | async-start | bytes 65536 | tf_op jit(solution)/shard_map/all_to_all | solution.py:58
  118.5 150.6 %all-to-all-start.2 = ((bf16[256,6,2880]{2,1,0:T(8,128)(2,1)}), bf16[256,6,2880]{2,1,0:T(8,128)(2,1)}, u32[]{:S(2)}, u32[]{:S(2)}) async-start(bf16[256,6,2880]{2,1,0:T(8,128)(2,1)} %bitcast.42), calls=%async_computation.2 | async-start | bytes 24117248 | tf_op jit(solution)/shard_map/all_to_all | solution.py:10
  124.7 3.0 copy-start.3
  124.7 434.6 %reduce-scatter.2.cloned.1.call-start = ((), (), s32[]{:S(2)}) async-start(), calls=%async_computation.5 | async-start | bytes 15073280 | tf_op jit(solution)/shard_map/reduce_scatter | solution.py:85
  419.0 151.3 %copy-start.2 = (f32[64,4]{0,1:T(4,128)S(1)}, f32[64,4]{0,1:T(4,128)}, u32[]{:S(2)}) copy-start(f32[64,4]{0,1:T(4,128)} %param.10) | copy-start | bytes 3076
  559.3 81.8 %all-to-all-start.3 = ((bf16[64,6,2880]{2,1,0:T(8,128)(2,1)}), bf16[64,6,2880]{2,1,0:T(8,128)(2,1)}, u32[]{:S(2)}, u32[]{:S(2)}) async-start(bf16[64,6,2880]{2,1,0:T(8,128)(2,1)} %reduce-scatter.2.cloned.1.call-done), calls=%async_computation.4 | async-start | bytes 6029312 | tf_op jit(solution)/shard_map/all_to_all | solution.py:88
  644.5 8.3 %copy-start.1 = (bf16[64,2880]{1,0:T(8,128)(2,1)S(1)}, bf16[64,2880]{1,0:T(8,128)(2,1)}, u32[]{:S(2)}) copy-start(bf16[64,2880]{1,0:T(8,128)(2,1)} %param.8) | copy-start | bytes 1105924
Sparse Core Ops, SparseCore 0:
  419.1 140.2 reduce-scatter.1
